TPU v7x, 32 devices: a whole 2x2x4 slice. The times are simulated.
32 devices in a mesh: ang: 8 (over z, x), tile: 4 (over y, core).
Axes of the slice: x: 2, y: 2, z: 4, core: 2. Of those that a mesh axis runs over, the one named last changes fastest.
Arguments:
- sinogram: float32 [2, 64, 2048], P(None, 'ang'), may hold values from -6 to 6
- ray_offsets: int32 [64, 256], P('ang'), may hold values from 0 to 2047
- merge_matrices: float32 [3, 2, 2, 256, 256], replicated, may hold values from -1 to 1.5, as said below
Outputs:
- reconstruction: float32 [2, 2048, 2048], P(None, 'ang')
Inputs may be any that keep to these rules, and one draw needn't show every extreme that they name: merge_matrices[l, b, k] is zero outside the columns b * (96) to b * 96 + 256 / 2 + 31.
All inputs are finite; a program needn't handle non-finite values.
Results may differ from a plain program's by a relative error of at most 0.0003.
Values sent between devices are 32-bit elements; how exact they have to be, the bound alone decides.
A program may use at most 768 MiB of HBM per device.

v0:
```python
import math

import jax
import jax.numpy as jnp
from jax import lax
from jax.sharding import PartitionSpec as P


def partner_2(array, axis, bit):
    return lax.ppermute(array, axis, [(i, i ^ 1 << bit) for i in range(lax.axis_size(axis))])


def apply_rows(matrix, field):
    return jnp.einsum("rk,skc->src", matrix, field, precision=lax.Precision.HIGHEST)


def smear_rows(sinogram, offsets, first_col, tile_cols):
    slices = sinogram.shape[0]
    angles = sinogram.shape[1]
    bin_count = sinogram.shape[2]
    row_count = offsets.shape[1]
    blocks = angles // 8
    doubled = jnp.concatenate([sinogram, sinogram], axis=2)
    grouped = doubled.reshape(slices, blocks, 8, 2 * bin_count).transpose(1, 2, 0, 3)
    starts = jnp.remainder(offsets + first_col, bin_count)
    grouped_starts = starts.reshape(blocks, 8, row_count)

    def window(angle_rows, start):
        return lax.dynamic_slice_in_dim(angle_rows, start, tile_cols, 1)

    by_rows = jax.vmap(window, in_axes=(None, 0))
    by_angles = jax.vmap(by_rows, in_axes=(0, 0))

    def add_block(running, inputs):
        rows_block, start_block = inputs
        samples = by_angles(rows_block, start_block)
        return (running + jnp.sum(samples, axis=0), None)

    zeros_init = jnp.zeros((row_count, slices, tile_cols), jnp.float32)
    running, _ = lax.scan(add_block, zeros_init, (grouped, grouped_starts))
    return running.transpose(1, 0, 2) / math.sqrt(angles)


def body(sinogram, ray_offsets, merge_matrices):
    row_count = ray_offsets.shape[1]
    margin = row_count // 8
    width = row_count // 2 + margin
    tile_cols = sinogram.shape[2] // lax.axis_size("tile")
    first_col = lax.axis_index("tile") * tile_cols
    partial_value = smear_rows(sinogram, ray_offsets, first_col, tile_cols)
    own_index = lax.axis_index("ang")
    levels = lax.axis_size("ang").bit_length() - 1
    for level_num in range(levels):
        bit_num = levels - 1 - level_num
        own_bit = jnp.right_shift(own_index, bit_num) & 1
        own_matrix = merge_matrices[level_num, own_bit, 0]
        other_matrix = merge_matrices[level_num, own_bit, 1]
        send_start = (1 - own_bit) * (row_count // 2 - margin)
        sent_rows = lax.dynamic_slice_in_dim(partial_value, send_start, width, 1)
        partner = partner_2(sent_rows, "ang", bit_num)
        read_start = own_bit * (row_count // 2 - margin)
        band_matrix = lax.dynamic_slice_in_dim(other_matrix, read_start, width, 1)
        partial_value = apply_rows(own_matrix, partial_value) + apply_rows(band_matrix, partner)
    return lax.all_gather(partial_value, "tile", axis=2, tiled=True)


def solution(mesh):
    placed = (P(None, "ang", None), P("ang", None), P())
    return jax.shard_map(
        body, mesh=mesh, in_specs=placed, out_specs=P(None, "ang", None), check_vma=False
    )
```

profile of v0, /device:TPU:0, one launch (start us, length us, event | category | flops | bytes accessed | tf_op | source)
XLA Modules:
  0.0 1160.7 jit_solution(3746597719928638852)
XLA Ops:
  6.5 0.0 copy-start
  6.5 0.0 all-gather.2.cloned.1.call-start
  6.5 0.9 fusion.24
  7.4 1.1 pad_maximum_fusion
  8.5 8.9 copy.11
  17.3 798.0 %gather_fusion = f32[2048,2,512]{1,0,2:T(8,128)} fusion(f32[8,2,4096]{1,0,2:T(8,128)} %bitcast.69, s32[2048]{0:T(1024)S(1)} %bitcast.70), kind=kCustom, calls=%fused_computation | custom fusion | bytes 16801792 | tf_op jit(solution)/shard_map/while/body/eval_jaxpr/vmap(vmap())/gather | solution.py:29
  815.4 178.7 %reduce_sum.10 = f32[256,2,512]{1,0,2:T(8,128)} reduce(f32[8,256,2,512]{2,1,0,3:T(8,128)} %bitcast.4, f32[]{:T(128)} %constant.137.clone.1), dimensions={0}, to_apply=%region_0.1 | reduce | flops 1835008 | bytes 9437188 | tf_op jit(solution)/shard_map/while/body/eval_jaxpr/reduce_sum | solution.py:37
  994.1 37.8 %copy.12 = f32[256,2,512]{2,0,1:T(8,128)} copy(f32[256,2,512]{1,0,2:T(8,128)} %reduce_sum.10) | data formatting | bytes 2097152 | tf_op jit(solution)/shard_map/while/body/eval_jaxpr/reduce_sum | solution.py:37
  1031.9 2.3 broadcast_multiply_fusion
  1034.2 2.0 dynamic-slice_bitcast_fusion.2
  1036.2 0.8 collective-permute-start
  1037.0 0.0 copy-done
  1037.0 2.3 fusion.5
  1039.4 28.4 %collective-permute-done = f32[2,160,512]{2,1,0:T(8,128)} collective-permute-done((f32[2,160,512]{2,1,0:T(8,128)}, f32[2,160,512]{2,1,0:T(8,128)}, u32[]{:S(2)}, u32[]{:S(2)}) %collective-permute-start) | collective-permute-done | bytes 655392 | tf_op jit(solution)/shard_map/ppermute | solution.py:10
  1067.8 2.1 convolution_add_fusion.2
  1069.9 0.0 copy-start.1
  1069.9 1.0 copy-done.1
  1070.9 0.9 dynamic-slice_bitcast_fusion.1
  1071.8 0.2 collective-permute-start.1
  1071.9 2.3 fusion.3
  1074.2 13.3 %collective-permute-done.1 = f32[2,160,512]{2,1,0:T(8,128)} collective-permute-done((f32[2,160,512]{2,1,0:T(8,128)}, f32[2,160,512]{2,1,0:T(8,128)}, u32[]{:S(2)}, u32[]{:S(2)}) %collective-permute-start.1) | collective-permute-done | bytes 655392 | tf_op jit(solution)/shard_map/ppermute | solution.py:10
  1087.6 2.1 convolution_add_fusion.1
  1089.7 0.0 copy-start.2
  1089.7 1.0 copy-done.2
  1090.7 0.9 dynamic-slice_bitcast_fusion
  1091.6 1.5 collective-permute-start.2
  1093.0 3.0 fusion.1
  1096.1 10.9 collective-permute-done.2
  1106.9 4.0 fusion
  1110.9 0.0 all-gather.2.cloned.1.call-update
  1110.9 37.5 %all-gather.2.cloned.1.call-done = f32[2,256,2048]{1,2,0:T(8,128)} async-done(((f32[2,256,512]{1,2,0:T(8,128)}), f32[2,256,2048]{1,2,0:T(8,128)}) %all-gather.2.cloned.1.call-update) | async-done | bytes 4194320 | tf_op jit(solution)/shard_map/all_gather | solution.py:64
  1148.5 5.3 copy.17
  (1 shorter events, 0.0 us)
Async XLA Ops:
  6.5 1030.5 %copy-start = (f32[3,2,2,256,256]{4,3,2,1,0:T(8,128)S(1)}, f32[3,2,2,256,256]{4,3,2,1,0:T(8,128)}, u32[]{:S(2)}) copy-start(f32[3,2,2,256,256]{4,3,2,1,0:T(8,128)} %param.5) | copy-start | bytes 9437188
  6.5 1141.9 %all-gather.2.cloned.1.call-start = ((), (), s32[]{:S(2)}) async-start(), calls=%async_computation | async-start | bytes 5242880 | tf_op jit(solution)/shard_map/all_gather | solution.py:64
  1036.2 31.6 %collective-permute-start = (f32[2,160,512]{2,1,0:T(8,128)}, f32[2,160,512]{2,1,0:T(8,128)}, u32[]{:S(2)}, u32[]{:S(2)}) collective-permute-start(f32[2,160,512]{2,1,0:T(8,128)} %dynamic-slice_bitcast_fusion.2), channel_id=1, source_target_pairs={{0,16},{4,20},{8,24},{12,28},{16,0},{20,4},{24,8},{28,12},{1,17},{... | collective-permute-start | bytes 1966088 | tf_op jit(solution)/shard_map/ppermute | solution.py:10
  1069.9 1.0 copy-start.1
  1071.8 15.8 %collective-permute-start.1 = (f32[2,160,512]{2,1,0:T(8,128)}, f32[2,160,512]{2,1,0:T(8,128)}, u32[]{:S(2)}, u32[]{:S(2)}) collective-permute-start(f32[2,160,512]{2,1,0:T(8,128)} %dynamic-slice_bitcast_fusion.1), channel_id=1, source_target_pairs={{0,8},{4,12},{8,0},{12,4},{16,24},{20,28},{24,16},{28,20},{1,9},{5... | collective-permute-start | bytes 1966088 | tf_op jit(solution)/shard_map/ppermute | solution.py:10
  1089.7 1.0 copy-start.2
  1091.6 15.3 %collective-permute-start.2 = (f32[2,160,512]{2,1,0:T(8,128)}, f32[2,160,512]{2,1,0:T(8,128)}, u32[]{:S(2)}, u32[]{:S(2)}) collective-permute-start(f32[2,160,512]{2,1,0:T(8,128)} %dynamic-slice_bitcast_fusion), channel_id=1, source_target_pairs={{0,4},{4,0},{8,12},{12,8},{16,20},{20,16},{24,28},{28,24},{1,5},{5... | collective-permute-start | bytes 1966088 | tf_op jit(solution)/shard_map/ppermute | solution.py:10
Sparse Core Ops, SparseCore 0:
  1111.0 37.3 all-gather.1
where the time goes:
time: 1160 us
  local copies, waits for them, and re-layouts  856 us (74%)
  other arithmetic  183 us (16%)
  waiting for transfers between devices  90.1 us (8%)
  matrix products  15.9 us (1%)
  between operations  13.5 us (1%)
    gather x1, local copies, waits for them, and re-layouts, window(): return lax.dynamic_slice_in_dim(angle_rows, start, tile_cols, 1)  798 us
    reduce_sum x1, other arithmetic, add_block(): return (running + jnp.sum(samples, axis=0), None)  179 us
    ppermute x3, waiting for transfers between devices, partner_2(): lax.ppermute(array, axis, [(i, i ^ 1 << bit) for i in range(lax.axis_size...  52.6 us
    reduce_sum x1, local copies, waits for them, and re-layouts, add_block(): return (running + jnp.sum(samples, axis=0), None)  37.8 us
    all_gather x1, waiting for transfers between devices, body(): return lax.all_gather(partial_value, 'tile', axis=2, tiled=True)  37.5 us
  transfers between devices with their start and end apart: 4, of which 4 were waited for; matrix products, arithmetic and copies ran while one was open for 1% of the time, Pallas kernels for 0%

commit v1 on v0

v1 whole, which is shorter than its diff:
```python
import functools
import math

import jax
import jax.numpy as jnp
from jax import lax
from jax.experimental import pallas as pl
from jax.experimental.pallas import tpu as pltpu
from jax.sharding import PartitionSpec as P

LANES = 128
SUBLANES = 8
UNROLL = 4


def split_bf16(value):
    high = value.astype(jnp.bfloat16)
    return high, (value - high.astype(jnp.float32)).astype(jnp.bfloat16)


def merge_kernel(dims, starts_ref, groups_ref, row0_ref, tiles_ref, weights_ref, out_ref, wide_ref, samples_ref):
    slices, bins, angles, rows, width, groups = dims
    per_tile = SUBLANES // slices
    count = bins // LANES // per_tile
    spread = wide_ref.shape[0] // (groups * angles)

    def widen(angle, carry):
        for i in range(count):
            tile = tiles_ref[angle * count + i]
            for u in range(spread // count):
                turn = (-slices * u) % SUBLANES
                turned = pltpu.roll(tile, turn, 0) if turn else tile
                wide_ref[angle * spread + u * count + i] = turned
        return carry

    lax.fori_loop(0, groups * angles, widen, 0)
    lane = lax.broadcasted_iota(jnp.int32, (SUBLANES, LANES), 1)
    row0 = row0_ref[0]

    def by_group(index, carry):
        group = groups_ref[index]

        def by_rows(step, inner):
            for u in range(UNROLL):
                q = step * UNROLL + u
                sums = [None] * count
                for a in range(angles):
                    angle = group * angles + a
                    start = starts_ref[angle * rows + row0 + q]
                    base = angle * spread + lax.shift_right_logical(start, 7)
                    fine = jnp.bitwise_and(start, LANES - 1)
                    turn = jnp.bitwise_and(LANES - fine, LANES - 1)
                    mask = lane >= fine
                    held = [wide_ref[base + i] for i in range(count + 1)]
                    for i in range(count):
                        moved = pltpu.roll(jnp.where(mask, held[i], held[i + 1]), turn, 1)
                        sums[i] = moved if a == 0 else sums[i] + moved
                for i in range(count):
                    at = ((index * width + q) * count + i) * SUBLANES
                    samples_ref[pl.ds(pl.multiple_of(at, SUBLANES), SUBLANES), :] = sums[i]
            return inner

        return lax.fori_loop(0, width // UNROLL, by_rows, carry)

    lax.fori_loop(0, groups, by_group, 0)
    high, low = split_bf16(weights_ref[...])
    depth = groups * width
    pairs = bins // (2 * LANES)

    def by_columns(n, carry):
        s = n // pairs
        c0 = (n % pairs) * 2
        first = (c0 % count) * SUBLANES + (c0 // count) * slices + s
        parts = [samples_ref[pl.ds(first + k * SUBLANES, depth, stride=count * SUBLANES), :] for k in range(2)]
        field_high, field_low = split_bf16(jnp.concatenate(parts, axis=1))
        dot = functools.partial(jnp.dot, preferred_element_type=jnp.float32)
        total = dot(high, field_high) + (dot(high, field_low) + dot(low, field_high))
        out_ref[s, :, pl.ds(pl.multiple_of(c0 * LANES, 2 * LANES), 2 * LANES)] = total
        return carry

    lax.fori_loop(0, slices * pairs, by_columns, 0)


def body(sinogram, ray_offsets, merge_matrices):
    slices, angles, bins = sinogram.shape
    rows = ray_offsets.shape[1]
    margin = rows // 8
    width = rows // 2 + margin
    groups = lax.axis_size("ang")
    levels = groups.bit_length() - 1
    own = lax.axis_index("ang")
    per_tile = SUBLANES // slices
    count = bins // LANES // per_tile
    spread = count * (per_tile + 1)

    own_tiles = sinogram.reshape(slices, angles, per_tile, count, LANES).transpose(1, 3, 2, 0, 4)
    own_tiles = own_tiles.reshape(angles * count, SUBLANES, LANES)
    tiles = lax.all_gather(own_tiles, "ang", axis=0, tiled=True)
    starts = lax.all_gather(ray_offsets.reshape(-1), "ang", axis=0, tiled=True)

    bits = [jnp.right_shift(own, levels - 1 - level) & 1 for level in range(levels)]
    weights = None
    for level in range(levels - 1, -1, -1):
        matrices = lax.dynamic_index_in_dim(merge_matrices[level], bits[level], 0, keepdims=False)
        if level == 0:
            matrices = lax.dynamic_slice_in_dim(matrices, bits[0] * (rows // 2 - margin), width, 2)
        if weights is None:
            weights = matrices.transpose(1, 0, 2)
        else:
            weights = jnp.einsum("rxk,mkj->rxmj", weights, matrices, precision=lax.Precision.HIGHEST)
        weights = weights.reshape(rows, -1, matrices.shape[2])
    weights = weights.reshape(rows, groups * width) / math.sqrt(angles)

    flips = [int(format(i, f"0{levels}b")[::-1], 2) for i in range(groups)]
    group_order = jnp.bitwise_xor(own, jnp.array(flips, jnp.int32)).astype(jnp.int32)
    row0 = (bits[0] * (rows // 2 - margin)).astype(jnp.int32).reshape(1)

    smem = pl.BlockSpec(memory_space=pltpu.SMEM)
    vmem = pl.BlockSpec(memory_space=pltpu.VMEM)
    return pl.pallas_call(
        functools.partial(merge_kernel, (slices, bins, angles, rows, width, groups)),
        out_shape=jax.ShapeDtypeStruct((slices, rows, bins), jnp.float32),
        in_specs=[smem, smem, smem, vmem, vmem],
        out_specs=vmem,
        scratch_shapes=[
            pltpu.VMEM((groups * angles * spread, SUBLANES, LANES), jnp.float32),
            pltpu.VMEM((groups * width * count * SUBLANES, LANES), jnp.float32),
        ],
        compiler_params=pltpu.CompilerParams(vmem_limit_bytes=60 * 1024 * 1024),
    )(starts, group_order, row0, tiles, weights)


def solution(mesh):
    placed = (P(None, "ang", None), P("ang", None), P())
    return jax.shard_map(
        body, mesh=mesh, in_specs=placed, out_specs=P(None, "ang", None), check_vma=False
    )
```

time: 1160 us -> 152 us (0.13)
  local copies, waits for them, and re-layouts: 856 us -> 6.08 us
  other arithmetic: 183 us -> 0.6 us
  Pallas kernels: 0 us -> 92.7 us
  waiting for transfers between devices: 90.1 us -> 2.47 us
  blocking collectives: 0 us -> 34.5 us
  matrix products: 15.9 us -> 2.49 us
    gather x1 -> x0, local copies, waits for them, and re-layouts: 798 us -> none  [window(): return lax.dynamic_slice_in_dim(angle_rows, start, tile_cols, 1)]
    reduce_sum x1 -> x0, other arithmetic: 179 us -> none  [add_block(): return (running + jnp.sum(samples, axis=0), None)]
    pallas_call x0 -> x1, Pallas kernels: none -> 92.7 us  [body(): pl.pallas_call(functools.partial(merge_kernel, (slices, bins, angles, row...]
    ppermute x3 -> x0, waiting for transfers between devices: 52.6 us -> none  [partner_2(): lax.ppermute(array, axis, [(i, i ^ 1 << bit) for i in range(lax.axis_size...]
    reduce_sum x1 -> x0, local copies, waits for them, and re-layouts: 37.8 us -> none  [add_block(): return (running + jnp.sum(samples, axis=0), None)]
    all_gather x1, waiting for transfers between devices: 37.5 us -> 2.46 us  [body(): tiles = lax.all_gather(own_tiles, 'ang', axis=0, tiled=True)]
    all_gather x0 -> x1, blocking collectives: none -> 34.5 us  [body(): starts = lax.all_gather(ray_offsets.reshape(-1), 'ang', axis=0, tiled=True)]
    dot_general x6 -> x2, matrix products: 15.9 us -> 2.49 us  [body(): jnp.einsum('rxk,mkj->rxmj', weights, matrices, precision=lax.Precision.HI...]
  transfers between devices with their start and end apart: 4 -> 1, of which waited for: 4 -> 1; matrix products, arithmetic and copies ran while one was open for 1% -> 5% of each run, Pallas kernels for 0% -> 0%
where the time goes in v1:
time: 152 us
  Pallas kernels  92.7 us (61%)
  blocking collectives  34.5 us (23%)
  between operations  13.4 us (9%)
  local copies, waits for them, and re-layouts  6.08 us (4%)
  matrix products  2.49 us (2%)
  waiting for transfers between devices  2.47 us (2%)
    pallas_call x1, Pallas kernels, body(): pl.pallas_call(functools.partial(merge_kernel, (slices, bins, angles, row...  92.7 us
    all_gather x1, blocking collectives, body(): starts = lax.all_gather(ray_offsets.reshape(-1), 'ang', axis=0, tiled=True)  34.5 us
  transfers between devices with their start and end apart: 1, of which 1 were waited for; matrix products, arithmetic and copies ran while one was open for 5% of the time, Pallas kernels for 0%

profile of v1, /device:TPU:0, one launch (start us, length us, event | category | flops | bytes accessed | tf_op | source)
XLA Modules:
  0.0 152.2 jit_solution(9741927890102358148)
XLA Ops:
  6.5 0.0 all-gather.2.cloned.1.call-start
  6.5 1.7 %copy.11 = f32[2,8,4,4,128]{4,0,2,3,1:T(2,128)} copy(f32[2,8,4,4,128]{4,1,3,2,0:T(8,128)} %bitcast.37) | data formatting | bytes 262144 | tf_op jit(solution)/shard_map/reshape | solution.py:96
  8.2 0.0 all-gather.2.cloned.1.call-update
  8.2 0.7 copy.16
  8.9 2.2 %fusion.9 = (f32[1,2,2,256,256]{4,3,2,1,0:T(8,128)S(1)}, f32[1,2,2,256,256]{4,3,2,1,0:T(8,128)S(1)}, f32[1,2,2,256,256]{4,3,2,1,0:T(8,128)S(1)}) fusion(f32[3,2,2,256,256]{4,3,2,1,0:T(8,128)} %param.6), kind=kLoop, calls=%fused_computation.11 | loop fusion | bytes 6291456 | tf_op jit(solution)/shard_map/slice | solution.py:104
  11.2 1.0 fusion.1
  12.2 1.5 convolution_multiply_fusion
  13.7 0.0 copy-start
  13.7 1.5 copy.13.weights_ref
  15.2 34.5 %all_gather.6.starts_ref = s32[16384]{0:T(1024)} all-gather(s32[2048]{0:T(1024)S(1)} %bitcast.38), channel_id=1, replica_groups=mesh['ang'=8,'tile'=4] {'ang'}, dimensions={0}, use_global_device_ids=true | all-gather | bytes 73728 | tf_op jit(solution)/shard_map/all_gather | solution.py:99
  49.6 0.0 copy-done
  49.6 0.6 broadcast_xor_fusion.groups_ref
  50.2 2.5 %all-gather.2.cloned.1.call-done.tiles_ref = f32[256,8,128]{2,1,0:T(8,128)} async-done(((f32[32,8,128]{2,1,0:T(8,128)}), f32[256,8,128]{2,1,0:T(8,128)}) %all-gather.2.cloned.1.call-update) | async-done | bytes 1048592 | tf_op jit(solution)/shard_map/all_gather | solution.py:98
  52.7 92.7 %shard_map.46 = f32[2,256,2048]{2,1,0:T(8,128)} custom-call(s32[16384]{0:T(1024)} %all_gather.6.starts_ref, s32[8]{0:T(128)} %broadcast_xor_fusion.groups_ref, s32[1]{0:T(128)} %bitcast.row0_ref, f32[256,8,128]{2,1,0:T(8,128)} %all-gather.2.cloned.1.call-done.tiles_ref, f32[256,1280]{1,0:T(8,128)} %copy.13.weights_ref), custom_call_target="tpu_custom_call" | custom-call | tf_op jit(solution)/shard_map/pallas_call | solution.py:120
Async XLA Ops:
  6.5 46.2 %all-gather.2.cloned.1.call-start = ((), (), s32[]{:S(2)}) async-start(), calls=%async_computation | async-start | bytes 1179648 | tf_op jit(solution)/shard_map/all_gather | solution.py:98
  13.7 36.0 %copy-start = (s32[8]{0:T(128)S(1)}, s32[8]{0:T(128)}, u32[]{:S(2)}) copy-start(s32[8]{0:T(128)} %constant.56.clone) | copy-start | bytes 100
Sparse Core Ops, SparseCore 0:
  9.5 43.1 all-gather.1

commit v2 on v1

v2 whole, which is shorter than its diff:
```python
import functools
import math

import jax
import jax.numpy as jnp
from jax import lax
from jax.experimental import pallas as pl
from jax.experimental.pallas import tpu as pltpu
from jax.sharding import PartitionSpec as P

LANES = 128
SUBLANES = 8
UNROLL = 20


def gather_kernel(groups, tiles_ref, starts_ref, all_tiles_ref, all_starts_ref, send_sems, recv_sems, own_sems):
    own = lax.axis_index("ang")
    barrier = pltpu.get_barrier_semaphore()
    for k in range(1, groups):
        pl.semaphore_signal(barrier, inc=1, device_id={"ang": own ^ k}, device_id_type=pl.DeviceIdType.MESH)
    pl.semaphore_wait(barrier, groups - 1)
    pairs = ((starts_ref, all_starts_ref), (tiles_ref, all_tiles_ref))
    copies = []
    for k in range(1, groups):
        for n, (source, target) in enumerate(pairs):
            copies.append(
                pltpu.make_async_remote_copy(
                    src_ref=source,
                    dst_ref=target.at[own],
                    send_sem=send_sems.at[n, k],
                    recv_sem=recv_sems.at[n, k],
                    device_id={"ang": own ^ k},
                    device_id_type=pl.DeviceIdType.MESH,
                )
            )
    for n, (source, target) in enumerate(pairs):
        copies.append(pltpu.make_async_copy(source, target.at[own], own_sems.at[n]))
    for copy in copies:
        copy.start()
    for copy in copies:
        copy.wait()


def gather_groups(tiles, starts, groups):
    vmem = pl.BlockSpec(memory_space=pltpu.VMEM)
    sems = pltpu.SemaphoreType.DMA((2, groups))
    return pl.pallas_call(
        functools.partial(gather_kernel, groups),
        out_shape=[jax.ShapeDtypeStruct((groups,) + x.shape, x.dtype) for x in (tiles, starts)],
        in_specs=[vmem, vmem],
        out_specs=[vmem, vmem],
        scratch_shapes=[sems, sems, pltpu.SemaphoreType.DMA((2,))],
        compiler_params=pltpu.CompilerParams(collective_id=0, has_side_effects=True),
    )(tiles, starts)


def split_bf16(value):
    high = value.astype(jnp.bfloat16)
    return high, (value - high.astype(jnp.float32)).astype(jnp.bfloat16)


def merge_kernel(dims, starts_ref, groups_ref, row0_ref, tiles_ref, weights_ref, out_ref, wide_ref, samples_ref, high_ref, low_ref):
    slices, bins, angles, rows, width, groups = dims
    per_tile = SUBLANES // slices
    count = bins // LANES // per_tile
    spread = count * (per_tile + 1)

    def widen(angle, carry):
        for i in range(count):
            tile = tiles_ref[angle * count + i]
            for u in range(spread // count):
                turn = (-slices * u) % SUBLANES
                turned = pltpu.roll(tile, turn, 0) if turn else tile
                at = (angle * spread + u * count + i) * SUBLANES
                wide_ref[pl.ds(pl.multiple_of(at, SUBLANES), SUBLANES), :] = turned
        return carry

    lax.fori_loop(0, groups * angles, widen, 0)
    reverse_lane = LANES - 1 - lax.broadcasted_iota(jnp.int32, (SUBLANES, LANES), 1)
    row0 = row0_ref[0]
    unroll = math.gcd(width, UNROLL)

    def by_group(index, carry):
        group = groups_ref[index]

        def by_rows(step, inner):
            first = (2 * rows * group + row0 + step * unroll) * angles
            for u in range(unroll):
                q = step * unroll + u
                sums = [None] * count
                for a in range(angles):
                    turn = starts_ref[first + u * angles + a + angles * rows]
                    base = starts_ref[first + u * angles + a]
                    mask = reverse_lane < turn
                    held = []
                    for i in range(count + 1):
                        at = pl.multiple_of(base + i * SUBLANES, SUBLANES)
                        held.append(wide_ref[pl.ds(at, SUBLANES), :])
                    for i in range(count):
                        moved = pltpu.roll(jnp.where(mask, held[i], held[i + 1]), turn, 1)
                        sums[i] = moved if a == 0 else sums[i] + moved
                for i in range(count):
                    at = ((index * width + q) * count + i) * SUBLANES
                    samples_ref[pl.ds(pl.multiple_of(at, SUBLANES), SUBLANES), :] = sums[i]
            return inner

        return lax.fori_loop(0, width // unroll, by_rows, carry)

    lax.fori_loop(0, groups, by_group, 0)
    high_ref[...], low_ref[...] = split_bf16(weights_ref[...])
    depth = groups * width
    pairs = bins // (2 * LANES)

    def by_columns(n, carry):
        s = n // pairs
        c0 = (n % pairs) * 2
        first = (c0 % count) * SUBLANES + (c0 // count) * slices + s
        parts = [samples_ref[pl.ds(first + k * SUBLANES, depth, stride=count * SUBLANES), :] for k in range(2)]
        field_high, field_low = split_bf16(jnp.concatenate(parts, axis=1))
        dot = functools.partial(jnp.dot, preferred_element_type=jnp.float32)
        total = dot(high_ref[...], field_high) + (dot(high_ref[...], field_low) + dot(low_ref[...], field_high))
        out_ref[s, :, pl.ds(pl.multiple_of(c0 * LANES, 2 * LANES), 2 * LANES)] = total
        return carry

    lax.fori_loop(0, slices * pairs, by_columns, 0)


def body(sinogram, ray_offsets, merge_matrices):
    slices, angles, bins = sinogram.shape
    assert slices == 2 and lax.axis_size("tile") % 2 == 0
    rows = ray_offsets.shape[1]
    margin = rows // 8
    width = rows // 2 + margin
    groups = lax.axis_size("ang")
    levels = groups.bit_length() - 1
    own = lax.axis_index("ang")
    core = lax.axis_index("tile") % slices
    per_tile = SUBLANES
    count = bins // LANES // per_tile
    spread = count * (per_tile + 1)

    own_tiles = lax.dynamic_index_in_dim(sinogram, core, 0, keepdims=False)
    own_tiles = own_tiles.reshape(angles, per_tile, count, LANES).transpose(0, 2, 1, 3)
    own_tiles = own_tiles.reshape(angles * count, SUBLANES, LANES)
    angle = own * angles + jnp.arange(angles, dtype=jnp.int32)[:, None]
    bases = (angle * spread + jnp.right_shift(ray_offsets, 7)) * SUBLANES
    turns = LANES - jnp.bitwise_and(ray_offsets, LANES - 1)
    own_starts = jnp.stack([bases, turns]).transpose(0, 2, 1).reshape(-1, LANES).astype(jnp.int32)
    tiles, starts = gather_groups(own_tiles, own_starts, groups)
    tiles = tiles.reshape(-1, SUBLANES, LANES)
    starts = starts.reshape(-1)

    bits = [jnp.right_shift(own, levels - 1 - level) & 1 for level in range(levels)]
    weights = None
    for level in range(levels - 1, -1, -1):
        matrices = lax.dynamic_index_in_dim(merge_matrices[level], bits[level], 0, keepdims=False)
        if level == 0:
            matrices = lax.dynamic_slice_in_dim(matrices, bits[0] * (rows // 2 - margin), width, 2)
        if weights is None:
            weights = matrices.transpose(1, 0, 2)
        else:
            weights = jnp.einsum("rxk,mkj->rxmj", weights, matrices, precision=lax.Precision.HIGHEST)
        weights = weights.reshape(rows, -1, matrices.shape[2])
    weights = weights.reshape(rows, groups * width) / math.sqrt(angles)

    flips = [int(format(i, f"0{levels}b")[::-1], 2) for i in range(groups)]
    group_order = jnp.bitwise_xor(own, jnp.array(flips, jnp.int32)).astype(jnp.int32)
    row0 = (bits[0] * (rows // 2 - margin)).astype(jnp.int32).reshape(1)

    smem = pl.BlockSpec(memory_space=pltpu.SMEM)
    vmem = pl.BlockSpec(memory_space=pltpu.VMEM)
    finished = pl.pallas_call(
        functools.partial(merge_kernel, (1, bins, angles, rows, width, groups)),
        out_shape=jax.ShapeDtypeStruct((1, rows, bins), jnp.float32),
        in_specs=[smem, smem, smem, vmem, vmem],
        out_specs=vmem,
        scratch_shapes=[
            pltpu.VMEM((groups * angles * spread * SUBLANES, LANES), jnp.float32),
            pltpu.VMEM((groups * width * count * SUBLANES, LANES), jnp.float32),
            pltpu.VMEM((rows, groups * width), jnp.bfloat16),
            pltpu.VMEM((rows, groups * width), jnp.bfloat16),
        ],
        compiler_params=pltpu.CompilerParams(vmem_limit_bytes=60 * 1024 * 1024),
    )(starts, group_order, row0, tiles, weights)
    swaps = [(i, i ^ 1) for i in range(lax.axis_size("tile"))]
    other = lax.ppermute(finished, "tile", swaps)
    first = jnp.where(core == 0, finished, other)
    second = jnp.where(core == 0, other, finished)
    return jnp.concatenate([first, second], axis=0)


def solution(mesh):
    placed = (P(None, "ang", None), P("ang", None), P())
    return jax.shard_map(
        body, mesh=mesh, in_specs=placed, out_specs=P(None, "ang", None), check_vma=False
    )
```

time: 152 us -> 78.9 us (0.52)
  blocking collectives: 34.5 us -> 0 us
  Pallas kernels: 92.7 us -> 59.9 us
  between operations: 13.4 us -> 0.07 us
  other arithmetic: 0.6 us -> 6.28 us
  waiting for transfers between devices: 2.47 us -> 4.37 us
    all_gather x1 -> x0, blocking collectives: 34.5 us -> none  [body(): starts = lax.all_gather(ray_offsets.reshape(-1), 'ang', axis=0, tiled=True)]
    pallas_call x1 -> x2, Pallas kernels: 92.7 us -> 59.9 us  [the longest x1 39.2 us: body(): pl.pallas_call(functools.partial(merge_kernel, (1, bins, angles, rows, wi...]
    ppermute x0 -> x1, waiting for transfers between devices: none -> 4.37 us  [body(): other = lax.ppermute(finished, 'tile', swaps)]
    all_gather x1 -> x0, waiting for transfers between devices: 2.46 us -> none  [body(): tiles = lax.all_gather(own_tiles, 'ang', axis=0, tiled=True)]
    concatenate x0 -> x1, other arithmetic: none -> 2.28 us  [body(): return jnp.concatenate([first, second], axis=0)]
    select_n x0 -> x1, other arithmetic: none -> 2.02 us  [body(): first = jnp.where(core == 0, finished, other)]
  transfers between devices with their start and end apart: 1 -> 1, of which waited for: 1 -> 1; matrix products, arithmetic and copies ran while one was open for 5% -> 0% of each run, Pallas kernels for 0% -> 0%
where the time goes in v2:
time: 78.9 us; the launch traced here: 78.4 us
  Pallas kernels  59.9 us (76%)
  other arithmetic  6.28 us (8%)
  local copies, waits for them, and re-layouts  5.29 us (7%)
  waiting for transfers between devices  4.37 us (6%)
  matrix products  2.48 us (3%)
    pallas_call x1, Pallas kernels, body(): pl.pallas_call(functools.partial(merge_kernel, (1, bins, angles, rows, wi...  39.2 us
    pallas_call x1, Pallas kernels, gather_groups(): pl.pallas_call(functools.partial(gather_kernel, groups), out_shape=[jax.S...  20.7 us
    ppermute x1, waiting for transfers between devices, body(): other = lax.ppermute(finished, 'tile', swaps)  4.37 us
    dot_general x2, matrix products, body(): jnp.einsum('rxk,mkj->rxmj', weights, matrices, precision=lax.Precision.HI...  2.48 us
    concatenate x1, other arithmetic, body(): return jnp.concatenate([first, second], axis=0)  2.28 us
    slice x1, local copies, waits for them, and re-layouts, body(): merge_matrices[level]  2.23 us
    select_n x1, other arithmetic, body(): first = jnp.where(core == 0, finished, other)  2.02 us
  transfers between devices with their start and end apart: 1, of which 1 were waited for; matrix products, arithmetic and copies ran while one was open for 0% of the time, Pallas kernels for 0%

profile of v2, /device:TPU:0, one launch (start us, length us, event | category | flops | bytes accessed | tf_op | source)
XLA Modules:
  0.0 78.4 jit_solution(2141206326203565590)
XLA Ops:
  0.0 0.0 copy-start
  0.0 1.2 %broadcast_xor_fusion.groups_ref = s32[8]{0:T(128)} fusion(s32[8]{0:T(128)} %constant.83.clone, s32[]{:T(128)S(6)} %axis_index.25), kind=kLoop, calls=%fused_computation.18 | loop fusion | flops 8 | bytes 68 | tf_op jit(solution)/shard_map/xor | solution.py:167
  1.2 0.0 copy-done
  1.2 0.1 reshape.38
  1.3 0.6 copy.8
  1.9 0.8 multiply_bitcast_fusion
  2.7 0.1 copy.9
  2.8 0.8 reshape.40.starts_ref
  3.6 2.2 %fusion.9 = (f32[1,2,2,256,256]{4,3,2,1,0:T(8,128)S(1)}, f32[1,2,2,256,256]{4,3,2,1,0:T(8,128)S(1)}, f32[1,2,2,256,256]{4,3,2,1,0:T(8,128)S(1)}) fusion(f32[3,2,2,256,256]{4,3,2,1,0:T(8,128)} %param.6), kind=kLoop, calls=%fused_computation.19 | loop fusion | bytes 6291456 | tf_op jit(solution)/shard_map/slice | solution.py:156
  5.8 1.0 %fusion.1 = f32[256,2,2,256]{3,0,2,1:T(8,128)S(1)} fusion(f32[1,2,2,256,256]{4,3,2,1,0:T(8,128)S(1)} %get-tuple-element.13, s32[]{:T(128)S(6)} %select_n.44, f32[1,2,2,256,256]{4,3,2,1,0:T(8,128)S(1)} %get-tuple-element.12, s32[]{:T(128)S(6)} %select_n.43), kind=kOutput, calls=%fused_computation.5 | convolution fusion | flops 805306368 | bytes 2097160 | tf_op jit(solution)/shard_map/rxk,mkj->rxmj/dot_general | solution.py:162
  6.9 1.5 %convolution_multiply_fusion = f32[256,4,2,160]{0,3,2,1:T(8,128)S(1)} fusion(f32[256,4,256,1]{2,0,3,1:T(8,128)S(1)} %bitcast.39, f32[1,2,2,256,256]{4,3,2,1,0:T(8,128)S(1)} %get-tuple-element.11, s32[]{:T(128)S(6)} %select_n.46, s32[]{:T(128)S(6)} %select_n.48), kind=kOutput, calls=%fused_computation.1 | convolution fusion | flops 1006960640 | bytes 2883592 | tf_op jit(solution)/shard_map/rxk,mkj->rxmj/dot_general | solution.py:162
  8.3 1.5 %copy.11.weights_ref = f32[256,1280]{1,0:T(8,128)} copy(f32[256,1280]{0,1:T(8,128)S(1)} %bitcast.38) | data formatting | bytes 2621440 | tf_op jit(solution)/shard_map/div | solution.py:164
  9.8 20.7 %shard_map.46 = (f32[8,16,8,128]{3,2,1,0:T(8,128)}, s32[8,32,128]{2,1,0:T(8,128)}) custom-call(f32[16,8,128]{2,1,0:T(8,128)} %bitcast.41, s32[32,128]{1,0:T(8,128)} %reshape.40.starts_ref), custom_call_target="tpu_custom_call" | custom-call | tf_op jit(solution)/shard_map/pallas_call | solution.py:47
  30.5 39.2 %shard_map.47 = f32[1,256,2048]{2,1,0:T(8,128)} custom-call(s32[32768]{0:T(1024)} %bitcast.43, s32[8]{0:T(128)} %broadcast_xor_fusion.groups_ref, s32[1]{0:T(128)} %bitcast.6.row0_ref, f32[128,8,128]{2,1,0:T(8,128)} %bitcast.40, f32[256,1280]{1,0:T(8,128)} %copy.11.weights_ref), custom_call_target="tpu_custom_call" | custom-call | tf_op jit(solution)/shard_map/pallas_call | solution.py:172
  69.7 0.0 collective-permute-start
  69.7 4.4 %collective-permute-done = f32[1,256,2048]{2,1,0:T(8,128)S(1)} collective-permute-done((f32[1,256,2048]{2,1,0:T(8,128)}, f32[1,256,2048]{2,1,0:T(8,128)S(1)}, u32[]{:S(2)}, u32[]{:S(2)}) %collective-permute-start) | collective-permute-done | bytes 2097184 | tf_op jit(solution)/shard_map/ppermute | solution.py:186
  74.1 2.0 %broadcast_select_fusion.1 = (f32[1,256,2048]{2,1,0:T(8,128)S(1)}, f32[1,256,2048]{2,1,0:T(8,128)S(1)}) fusion(f32[1,256,2048]{2,1,0:T(8,128)} %shard_map.47, f32[1,256,2048]{2,1,0:T(8,128)S(1)} %collective-permute-done, pred[]{:T(512)S(6)} %eq.6), kind=kLoop, calls=%fused_computation.3 | loop fusion | flops 1048576 | bytes 8388609 | tf_op jit(solution)/shard_map/jit(_where)/select_n | solution.py:187
  76.1 2.3 %pad_maximum_fusion = f32[2,256,2048]{2,1,0:T(8,128)} fusion(f32[1,256,2048]{2,1,0:T(8,128)S(1)} %get-tuple-element.10, f32[1,256,2048]{2,1,0:T(8,128)S(1)} %get-tuple-element.9), kind=kLoop, calls=%fused_computation | loop fusion | flops 1048576 | bytes 8388608 | tf_op jit(solution)/shard_map/concatenate | solution.py:189
  (3 shorter events, 0.0 us)
Async XLA Ops:
  0.0 1.2 %copy-start = (f32[2,8,2048]{2,1,0:T(8,128)S(1)}, f32[2,8,2048]{2,1,0:T(8,128)}, u32[]{:S(2)}) copy-start(f32[2,8,2048]{2,1,0:T(8,128)} %param.4) | copy-start | bytes 393220
  69.7 4.4 %collective-permute-start = (f32[1,256,2048]{2,1,0:T(8,128)}, f32[1,256,2048]{2,1,0:T(8,128)S(1)}, u32[]{:S(2)}, u32[]{:S(2)}) collective-permute-start(f32[1,256,2048]{2,1,0:T(8,128)} %shard_map.47), channel_id=1, source_target_pairs={{0,1},{1,0},{2,3},{3,2},{4,5},{5,4},{6,7},{7,6},{8,9},{9,8},{10,11... | collective-permute-start | bytes 6291464 | tf_op jit(solution)/shard_map/ppermute | solution.py:186

commit v3 on v2

--- a/solution.py
+++ b/solution.py
@@ -10,7 +10,7 @@
 
 LANES = 128
 SUBLANES = 8
-UNROLL = 20
+UNROLL = 40
 
 
 def gather_kernel(groups, tiles_ref, starts_ref, all_tiles_ref, all_starts_ref, send_sems, recv_sems, own_sems):
@@ -184,9 +184,8 @@
     )(starts, group_order, row0, tiles, weights)
     swaps = [(i, i ^ 1) for i in range(lax.axis_size("tile"))]
     other = lax.ppermute(finished, "tile", swaps)
-    first = jnp.where(core == 0, finished, other)
-    second = jnp.where(core == 0, other, finished)
-    return jnp.concatenate([first, second], axis=0)
+    place = lax.broadcasted_iota(jnp.int32, (slices, 1, 1), 0)
+    return jnp.where(place == core, finished, other)
 
 
 def solution(mesh):

time: 78.9 us -> 76.5 us (0.970)
  Pallas kernels: 59.9 us -> 57.5 us
    pallas_call x1, Pallas kernels: 39.2 us -> 36.8 us  [body(): pl.pallas_call(functools.partial(merge_kernel, (1, bins, angles, rows, wi...]
    select_n x1, other arithmetic: 2.02 us -> 4.32 us  [body(): return jnp.where(place == core, finished, other)]
    concatenate x1 -> x0, other arithmetic: 2.28 us -> none  [body(): return jnp.concatenate([first, second], axis=0)]
where the time goes in v3:
time: 76.5 us; the launch traced here: 76 us
  Pallas kernels  57.5 us (75%)
  other arithmetic  6.3 us (8%)
  local copies, waits for them, and re-layouts  5.27 us (7%)
  waiting for transfers between devices  4.36 us (6%)
  matrix products  2.48 us (3%)
    pallas_call x1, Pallas kernels, body(): pl.pallas_call(functools.partial(merge_kernel, (1, bins, angles, rows, wi...  36.8 us
    pallas_call x1, Pallas kernels, gather_groups(): pl.pallas_call(functools.partial(gather_kernel, groups), out_shape=[jax.S...  20.7 us
    ppermute x1, waiting for transfers between devices, body(): other = lax.ppermute(finished, 'tile', swaps)  4.36 us
    select_n x1, other arithmetic, body(): return jnp.where(place == core, finished, other)  4.32 us
    dot_general x2, matrix products, body(): jnp.einsum('rxk,mkj->rxmj', weights, matrices, precision=lax.Precision.HI...  2.48 us
    slice x1, local copies, waits for them, and re-layouts, body(): merge_matrices[level]  2.23 us
  transfers between devices with their start and end apart: 1, of which 1 were waited for; matrix products, arithmetic and copies ran while one was open for 0% of the time, Pallas kernels for 0%

profile of v3, /device:TPU:0, one launch (start us, length us, event | category | flops | bytes accessed | tf_op | source)
XLA Modules:
  0.0 76.0 jit_solution(2242580719187695263)
XLA Ops:
  0.0 0.0 copy-start
  0.0 1.2 %broadcast_xor_fusion.groups_ref = s32[8]{0:T(128)} fusion(s32[8]{0:T(128)} %constant.83.clone, s32[]{:T(128)S(6)} %axis_index.25), kind=kLoop, calls=%fused_computation.17 | loop fusion | flops 8 | bytes 68 | tf_op jit(solution)/shard_map/xor | solution.py:167
  1.2 0.0 copy-done
  1.2 0.1 reshape.43
  1.3 0.6 copy.8
  1.9 0.8 %multiply_bitcast_fusion = (s32[1,8,256]{2,1,0:T(8,128)S(1)}, s32[1,8,256]{2,1,0:T(8,128)S(1)}) fusion(s32[8,256]{1,0:T(8,128)} %param.5, s32[8]{0:T(128)S(1)} %add_multiply_fusion), kind=kLoop, calls=%fused_computation.11 | loop fusion | flops 10240 | bytes 24608 | tf_op jit(solution)/shard_map/stack | solution.py:148
  2.7 0.1 copy.9
  2.8 0.7 reshape.45.starts_ref
  3.6 2.2 %fusion.9 = (f32[1,2,2,256,256]{4,3,2,1,0:T(8,128)S(1)}, f32[1,2,2,256,256]{4,3,2,1,0:T(8,128)S(1)}, f32[1,2,2,256,256]{4,3,2,1,0:T(8,128)S(1)}) fusion(f32[3,2,2,256,256]{4,3,2,1,0:T(8,128)} %param.6), kind=kLoop, calls=%fused_computation.18 | loop fusion | bytes 6291456 | tf_op jit(solution)/shard_map/slice | solution.py:156
  5.8 1.0 %fusion.1 = f32[256,2,2,256]{3,0,2,1:T(8,128)S(1)} fusion(f32[1,2,2,256,256]{4,3,2,1,0:T(8,128)S(1)} %get-tuple-element.11, s32[]{:T(128)S(6)} %select_n.35, f32[1,2,2,256,256]{4,3,2,1,0:T(8,128)S(1)} %get-tuple-element.10, s32[]{:T(128)S(6)} %select_n.34), kind=kOutput, calls=%fused_computation.3 | convolution fusion | flops 805306368 | bytes 2097160 | tf_op jit(solution)/shard_map/rxk,mkj->rxmj/dot_general | solution.py:162
  6.8 1.5 %convolution_multiply_fusion = f32[256,4,2,160]{0,3,2,1:T(8,128)S(1)} fusion(f32[256,4,256,1]{2,0,3,1:T(8,128)S(1)} %bitcast.42, f32[1,2,2,256,256]{4,3,2,1,0:T(8,128)S(1)} %get-tuple-element.9, s32[]{:T(128)S(6)} %select_n.37, s32[]{:T(128)S(6)} %select_n.39), kind=kOutput, calls=%fused_computation.1 | convolution fusion | flops 1006960640 | bytes 2883592 | tf_op jit(solution)/shard_map/rxk,mkj->rxmj/dot_general | solution.py:162
  8.3 1.5 %copy.11.weights_ref = f32[256,1280]{1,0:T(8,128)} copy(f32[256,1280]{0,1:T(8,128)S(1)} %bitcast.41) | data formatting | bytes 2621440 | tf_op jit(solution)/shard_map/div | solution.py:164
  9.8 20.7 %shard_map.46 = (f32[8,16,8,128]{3,2,1,0:T(8,128)}, s32[8,32,128]{2,1,0:T(8,128)}) custom-call(f32[16,8,128]{2,1,0:T(8,128)} %bitcast.45, s32[32,128]{1,0:T(8,128)} %reshape.45.starts_ref), custom_call_target="tpu_custom_call" | custom-call | tf_op jit(solution)/shard_map/pallas_call | solution.py:47
  30.4 36.8 %shard_map.47 = f32[1,256,2048]{2,1,0:T(8,128)} custom-call(s32[32768]{0:T(1024)} %bitcast.47, s32[8]{0:T(128)} %broadcast_xor_fusion.groups_ref, s32[1]{0:T(128)} %bitcast.6.row0_ref, f32[128,8,128]{2,1,0:T(8,128)} %bitcast.44, f32[256,1280]{1,0:T(8,128)} %copy.11.weights_ref), custom_call_target="tpu_custom_call" | custom-call | tf_op jit(solution)/shard_map/pallas_call | solution.py:172
  67.3 0.0 collective-permute-start
  67.3 4.4 %collective-permute-done = f32[1,256,2048]{2,1,0:T(8,128)S(1)} collective-permute-done((f32[1,256,2048]{2,1,0:T(8,128)}, f32[1,256,2048]{2,1,0:T(8,128)S(1)}, u32[]{:S(2)}, u32[]{:S(2)}) %collective-permute-start) | collective-permute-done | bytes 2097184 | tf_op jit(solution)/shard_map/ppermute | solution.py:186
  71.7 4.3 %broadcast_select_fusion = f32[2,256,2048]{2,1,0:T(8,128)} fusion(f32[256,2048]{1,0:T(8,128)S(1)} %bitcast.43, f32[256,2048]{1,0:T(8,128)} %bitcast.40, pred[2]{0:T(512)(128)(4,1)S(1)} %iota_compare_fusion), kind=kLoop, calls=%fused_computation | loop fusion | flops 1048576 | bytes 8388610 | tf_op jit(solution)/shard_map/jit(_where)/select_n | solution.py:188
  (4 shorter events, 0.0 us)
Async XLA Ops:
  0.0 1.2 %copy-start = (f32[2,8,2048]{2,1,0:T(8,128)S(1)}, f32[2,8,2048]{2,1,0:T(8,128)}, u32[]{:S(2)}) copy-start(f32[2,8,2048]{2,1,0:T(8,128)} %param.4) | copy-start | bytes 393220
  67.3 4.4 %collective-permute-start = (f32[1,256,2048]{2,1,0:T(8,128)}, f32[1,256,2048]{2,1,0:T(8,128)S(1)}, u32[]{:S(2)}, u32[]{:S(2)}) collective-permute-start(f32[1,256,2048]{2,1,0:T(8,128)} %shard_map.47), channel_id=1, source_target_pairs={{0,1},{1,0},{2,3},{3,2},{4,5},{5,4},{6,7},{7,6},{8,9},{9,8},{10,11... | collective-permute-start | bytes 6291464 | tf_op jit(solution)/shard_map/ppermute | solution.py:186
